TPU v7x, 32 devices: a whole 2x2x4 slice. The times are simulated.
32 devices in a mesh: seq: 8 (over z, x), head: 4 (over y, core).
Axes of the slice: x: 2, y: 2, z: 4, core: 2. Of those that a mesh axis runs over, the one named last changes fastest.
Arguments:
- context: bfloat16 [4, 4096, 1024], P('head', 'seq'), may hold values from -6 to 6
- latents: bfloat16 [4, 1024, 1024], P('head'), may hold values from -6 to 6
- offsets: int32 [4], P('head'), may hold values from 0 to 3072
- query_gain: float32 [1024], replicated, may hold values from 0.1 to 1.9
- key_gain: float32 [1024], replicated, may hold values from 0.1 to 1.9
- layer_gain: float32 [2, 1024], replicated, may hold values from 0.1 to 1.9
- cross_query: bfloat16 [1024, 1024], P(('seq', 'head')), may hold values from -0.25 to 0.25
- cross_key: bfloat16 [1024, 1024], P(('seq', 'head')), may hold values from -0.25 to 0.25
- cross_value: bfloat16 [1024, 1024], P(('seq', 'head')), may hold values from -0.1875 to 0.1875
- cross_out: bfloat16 [1024, 1024], P(('seq', 'head')), may hold values from -0.1875 to 0.1875
- layer_qkv: bfloat16 [2, 1024, 3072], P(None, ('seq', 'head')), may hold values from -0.25 to 0.25
- layer_out: bfloat16 [2, 1024, 1024], P(None, ('seq', 'head')), may hold values from -0.1875 to 0.1875
Outputs:
- latent_out: bfloat16 [4, 1024, 1024], P('head', 'seq')
Inputs may be any that keep to these rules, and one draw needn't show every extreme that they name: Latent i of row b stands at context position offsets[b] + i.
All inputs are finite; a program needn't handle non-finite values.
Results may differ from a plain program's by a relative error of at most 0.013.
Values may be sent and summed in bfloat16 or wider, within the bound.
No kernel may reach another device: no remote copies, remote signals or barrier semaphores. Data moves between devices by JAX's collectives and lax.ppermute only.
A program may use at most 128 MiB of HBM per device.

v0:
```python
import jax
import jax.numpy as jnp
from jax import lax
from jax.sharding import PartitionSpec as P

H = 16
EPSILON = 1e-06
NEGATIVE = -1e30


def rms_norm(value_matrix, gain):
    value_matrix = value_matrix.astype(jnp.float32)
    scale = lax.rsqrt(jnp.mean(value_matrix * value_matrix, axis=-1, keepdims=True) + EPSILON)
    return (value_matrix * scale * gain).astype(jnp.bfloat16)


def project(left, weight):
    return jnp.einsum("...k,kn->...n", left, weight, preferred_element_type=jnp.float32)


def block_scores(query_row_block, key_rows, query_pos, key_base, start, key_span, scale):
    key_tile = lax.dynamic_slice_in_dim(key_rows, start, key_span, 0)
    score_matrix = (
        jnp.einsum("oqi,cqi->qoc", query_row_block, key_tile, preferred_element_type=jnp.float32)
        * scale
    )
    key_pos = key_base + start + jnp.arange(key_span, dtype=jnp.int32)
    valid = key_pos[None, None, :] <= query_pos[None, :, None]
    return (jnp.where(valid, score_matrix, NEGATIVE), valid)


def causal_top(query_row_block, key_rows, query_pos, key_base, key_span, scale):

    def advance(index, best):
        start = index * key_span

        def compute(kept):
            score_matrix, valid = block_scores(
                query_row_block, key_rows, query_pos, key_base, start, key_span, scale
            )
            return jnp.maximum(kept, jnp.max(score_matrix, axis=2))

        result = compute(best)
        return result

    initial = jnp.full((query_row_block.shape[1], query_row_block.shape[0]), NEGATIVE, jnp.float32)
    return lax.fori_loop(0, key_rows.shape[0] // key_span, advance, initial)


def causal_sums(
    query_row_block, key_rows, value_rows, row_top, query_pos, key_base, key_span, scale
):

    def advance(index, carry):
        start = index * key_span

        def compute(kept):
            numerator_sum, denom = kept
            score_matrix, valid = block_scores(
                query_row_block, key_rows, query_pos, key_base, start, key_span, scale
            )
            probability_rows = jnp.where(
                valid, jnp.exp(score_matrix - row_top[:, :, None]), 0.0
            ).astype(jnp.bfloat16)
            value_tile = lax.dynamic_slice_in_dim(value_rows, start, key_span, 0)
            numerator_sum = numerator_sum + jnp.einsum(
                "ycv,vys->cys", probability_rows, value_tile, preferred_element_type=jnp.float32
            )
            denom = denom + jnp.transpose(jnp.sum(probability_rows.astype(jnp.float32), axis=2))
            return (numerator_sum, denom)

        result = compute(carry)
        return result

    count, heads, head_width = query_row_block.shape
    initial = (
        jnp.zeros((count, heads, head_width), jnp.float32),
        jnp.zeros((count, heads), jnp.float32),
    )
    return lax.fori_loop(0, key_rows.shape[0] // key_span, advance, initial)


def latent_attention(piece):
    count = piece.shape[1]
    head_width = piece.shape[-1]
    query_matrix = piece[:, :, 0]
    key_matrix = piece[:, :, 1]
    value_matrix = piece[:, :, 2]
    score_matrix = jnp.einsum(
        "bmhd,bkhd->bhmk", query_matrix, key_matrix, preferred_element_type=jnp.float32
    ) * head_width ** (-0.5)
    positions = jnp.arange(count, dtype=jnp.int32)
    valid = positions[None, :] <= positions[:, None]
    score_matrix = jnp.where(valid, score_matrix, NEGATIVE)
    row_top = jnp.max(score_matrix, axis=3, keepdims=True)
    probability_rows = jnp.where(valid, jnp.exp(score_matrix - row_top), 0.0).astype(jnp.bfloat16)
    denom = jnp.sum(probability_rows.astype(jnp.float32), axis=3)
    numerator_sum = jnp.einsum(
        "bhmk,bkhd->bmhd", probability_rows, value_matrix, preferred_element_type=jnp.float32
    )
    return (numerator_sum / jnp.transpose(denom, (0, 2, 1))[:, :, :, None]).astype(jnp.bfloat16)


def per_device(
    context,
    latents,
    offsets,
    query_gain,
    key_gain,
    layer_gain,
    cross_query,
    cross_key,
    cross_value,
    cross_out,
    layer_qkv,
    layer_out,
):
    batch, ctx_len, width = context.shape
    latent_count = latents.shape[1]
    heads = H
    head_width = width // heads
    groups = lax.axis_size("seq")
    local_rows = latent_count // groups
    group_heads = heads // groups
    seq_index = lax.axis_index("seq")
    scale = head_width ** (-0.5)
    gathered = (
        lax.all_gather(cross_query, ("seq", "head"), axis=0, tiled=True),
        lax.all_gather(cross_key, ("seq", "head"), axis=0, tiled=True),
        lax.all_gather(cross_value, ("seq", "head"), axis=0, tiled=True),
        lax.all_gather(cross_out, ("seq", "head"), axis=0, tiled=True),
        lax.all_gather(layer_qkv, ("seq", "head"), axis=1, tiled=True),
        lax.all_gather(layer_out, ("seq", "head"), axis=1, tiled=True),
    )
    normed_latents = rms_norm(latents, query_gain)
    query_matrix = project(normed_latents, gathered[0])
    query_matrix = query_matrix.astype(jnp.bfloat16)
    normed_context = rms_norm(context, key_gain)
    key_matrix = project(normed_context, gathered[1])
    value_matrix = project(normed_context, gathered[2])
    key_matrix = key_matrix.astype(jnp.bfloat16).reshape(batch, ctx_len, heads, head_width)
    value_matrix = value_matrix.astype(jnp.bfloat16).reshape(batch, ctx_len, heads, head_width)
    query_head_rows = query_matrix.reshape(batch, latent_count, heads, head_width)
    query_pos = offsets[:, None] + jnp.arange(latent_count, dtype=jnp.int32)[None, :]
    key_groups, value_groups = (
        lax.all_to_all(key_matrix, "seq", split_axis=2, concat_axis=1, tiled=True),
        lax.all_to_all(value_matrix, "seq", split_axis=2, concat_axis=1, tiled=True),
    )
    query_groups = lax.dynamic_slice_in_dim(
        query_head_rows, seq_index * group_heads, group_heads, 2
    )
    total_len = key_groups.shape[1]
    key_span = max(min(total_len, 512), total_len // 16)
    row_top = causal_top(query_groups[0], key_groups[0], query_pos[0], 0, key_span, scale)
    numerator_sum, denom = causal_sums(
        query_groups[0], key_groups[0], value_groups[0], row_top, query_pos[0], 0, key_span, scale
    )
    results = [(numerator_sum / denom[:, :, None]).astype(jnp.bfloat16)]
    attended = lax.all_to_all(
        jnp.stack(results), "seq", split_axis=1, concat_axis=2, tiled=True
    ).reshape(batch, local_rows, width)
    latents_own = lax.dynamic_slice_in_dim(latents, seq_index * local_rows, local_rows, 1)
    update = project(attended, gathered[3])
    hidden = (latents_own.astype(jnp.float32) + update).astype(jnp.bfloat16)
    for layer in range(layer_qkv.shape[0]):
        normed = rms_norm(hidden, layer_gain[layer])
        qkv = project(normed, gathered[4][layer])
        grouped = qkv.astype(jnp.bfloat16).reshape(batch, local_rows, 3, heads, head_width)
        mixed = latent_attention(
            lax.all_to_all(grouped, "seq", split_axis=3, concat_axis=1, tiled=True)
        )
        merged = lax.all_to_all(mixed, "seq", split_axis=1, concat_axis=2, tiled=True).reshape(
            batch, local_rows, width
        )
        update = project(merged, gathered[5][layer])
        hidden = (hidden.astype(jnp.float32) + update).astype(jnp.bfloat16)
    return hidden


def solution(mesh):
    return jax.shard_map(
        per_device,
        mesh=mesh,
        in_specs=(
            P("head", "seq", None),
            P("head", None, None),
            P("head"),
            P(),
            P(),
            P(),
            P(("seq", "head"), None),
            P(("seq", "head"), None),
            P(("seq", "head"), None),
            P(("seq", "head"), None),
            P(None, ("seq", "head"), None),
            P(None, ("seq", "head"), None),
        ),
        out_specs=P("head", "seq", None),
        check_vma=False,
    )
```

profile of v0, /device:TPU:0, one launch (start us, length us, event | category | flops | bytes accessed | tf_op | source)
XLA Modules:
  0.0 485.0 jit_solution(4928080488201104973)
XLA Ops:
  6.5 0.7 all-gather.9.cloned.1.call-update
  7.3 0.7 all-gather.7.cloned.1.call-update
  9.9 1.5 fusion.33
  11.4 57.8 %all-gather.9.cloned.1.call-done = bf16[1024,1024]{1,0:T(8,128)(2,1)} async-done(((bf16[32,1024]{1,0:T(8,128)(2,1)}), bf16[1024,1024]{1,0:T(8,128)(2,1)}) %all-gather.9.cloned.1.call-update) | async-done | bytes 2097168 | tf_op jit(solution)/shard_map/all_gather | solution.py:129
  69.2 3.2 convolution_convert_fusion
  72.4 1.3 copy.73
  73.8 4.3 all-to-all-start.1
  78.7 2.1 fusion.22
  80.8 51.9 %all-gather.7.cloned.1.call-done = bf16[1024,1024]{1,0:T(8,128)(2,1)} async-done(((bf16[32,1024]{1,0:T(8,128)(2,1)}), bf16[1024,1024]{1,0:T(8,128)(2,1)}) %all-gather.7.cloned.1.call-update) | async-done | bytes 2097168 | tf_op jit(solution)/shard_map/all_gather | solution.py:130
  132.7 3.9 convolution_convert_fusion.1
  136.6 2.3 copy.70
  138.9 51.8 %all-gather.11.cloned.1.call-done = bf16[1024,1024]{1,0:T(8,128)(2,1)} async-done(((bf16[32,1024]{1,0:T(8,128)(2,1)}), bf16[1024,1024]{1,0:T(8,128)(2,1)}) %all-gather.11.cloned.1.call-update) | async-done | bytes 2097168 | tf_op jit(solution)/shard_map/all_gather | solution.py:128
  190.7 4.8 fusion.43
  195.5 4.3 all-to-all-start
  199.9 1.6 copy.75
  201.4 1.6 squeeze.30
  203.0 16.9 %while.30 = (s32[]{:T(128)}, f32[2,1024]{1,0:T(2,128)S(1)}, bf16[4096,2,64]{0,2,1:T(8,128)(2,1)S(1)}, bf16[1024,2,64]{0,2,1:T(8,128)(2,1)S(1)}, s32[]{:T(128)}, ...) while((s32[]{:T(128)}, f32[2,1024]{1,0:T(2,128)S(1)}, bf16[4096,2,64]{0,2,1:T(8,128)(2,1)S(1)}, ...), condition=%wide.region_4.5_spmd.clone, body=%wide.region_2.4_spmd.clone.sunk | while | flops 137891328 | bytes 1487009 | solution.py:47
  204.0 1.0 fusion.103
  206.1 1.0 fusion.103
  208.3 1.0 fusion.103
  210.4 1.0 fusion.103
  212.5 1.0 fusion.103
  214.6 1.0 fusion.103
  216.7 1.0 fusion.103
  218.8 1.0 fusion.103
  219.9 8.5 %all-to-all-done = bf16[1,512,16,64]{1,3,0,2:T(8,128)(2,1)S(1)} async-done(((bf16[1,512,16,64]{1,3,0,2:T(8,128)(2,1)}), bf16[1,512,16,64]{1,3,0,2:T(8,128)(2,1)S(1)}, u32[]{:S(2)}, u32[]{:S(2)}) %all-to-all-start) | async-done | bytes 1048608 | tf_op jit(solution)/shard_map/all_to_all | solution.py:147
  228.9 1.3 squeeze.14
  230.2 40.6 %while.31 = (s32[]{:T(128)}, f32[1024,2,64]{0,2,1:T(8,128)S(1)}, f32[1024,2]{0,1:T(2,128)S(1)}, bf16[4096,2,64]{0,2,1:T(8,128)(2,1)}, bf16[4096,2,64]{0,2,1:T(8,...) while((s32[]{:T(128)}, f32[1024,2,64]{0,2,1:T(8,128)S(1)}, ...), condition=%wide.region_7.8_spmd.clone, body=%wide.region_5.7_spmd.clone.sunk | while | flops 276565504 | bytes 6869182 | solution.py:80
  231.3 2.5 convert_reduce_fusion.4
  233.8 1.4 fusion.107
  236.3 2.5 convert_reduce_fusion.4
  238.9 1.5 fusion.107
  241.5 2.5 convert_reduce_fusion.4
  244.0 1.4 fusion.107
  246.5 2.5 convert_reduce_fusion.4
  249.1 1.4 fusion.107
  251.6 2.5 convert_reduce_fusion.4
  254.1 1.4 fusion.107
  256.7 2.5 convert_reduce_fusion.4
  259.2 1.4 fusion.107
  261.7 2.5 convert_reduce_fusion.4
  264.3 1.5 fusion.107
  266.8 2.5 convert_reduce_fusion.4
  269.3 1.4 fusion.107
  271.6 1.1 reshape.307
  272.7 3.5 all-to-all-start.2
  276.3 9.1 %all-to-all-done.2 = bf16[8,2,8192]{2,1,0:T(2,128)(2,1)S(1)} async-done(((bf16[8,2,8192]{2,1,0:T(2,128)(2,1)}), bf16[8,2,8192]{2,1,0:T(2,128)(2,1)S(1)}, u32[]{:S(2)}, u32[]{:S(2)}) %all-to-all-start.2) | async-done | bytes 262176 | tf_op jit(solution)/shard_map/all_to_all | solution.py:159
  286.1 2.1 multiply_reduce_fusion.1
  288.3 64.0 %all-gather.15.cloned.1.call-done = bf16[2,1024,3072]{2,1,0:T(8,128)(2,1)} async-done(((bf16[2,32,3072]{2,1,0:T(8,128)(2,1)}), bf16[2,1024,3072]{2,1,0:T(8,128)(2,1)}) %all-gather.15.cloned.1.call-update) | async-done | bytes 12582928 | tf_op jit(solution)/shard_map/all_gather | solution.py:132
  352.3 3.8 fusion.31
  356.5 0.9 copy.82
  357.4 4.0 all-to-all-start.3
  361.8 23.0 %all-to-all-done.3 = bf16[1,128,3,16,64]{1,4,2,0,3:T(8,128)(2,1)S(1)} async-done(((bf16[1,128,3,16,64]{1,4,2,0,3:T(8,128)(2,1)}), bf16[1,128,3,16,64]{1,4,2,0,3:T(8,128)(2,1)S(1)}, u32[]{:S(2)}, u32[]{:S(2)}) %all-to-all-start.3) | async-done | bytes 786464 | tf_op jit(solution)/shard_map/all_to_all | solution.py:170
  385.6 6.0 %convert_reduce_fusion.2 = (f32[2,1024]{1,0:T(2,128)S(1)}, bf16[2,1024,1024]{1,2,0:T(8,128)(2,1)}) fusion(pred[1024,1024]{0,1:T(8,128)(4,1)S(1)} %iota_compare_fusion, bf16[1,1024,3,2,64]{1,4,3,2,0:T(8,128)(2,1)S(1)} %all_to_all.93), kind=kOutput, calls=%fused_computation.31 | convolution fusion | flops 283116544 | bytes 6823936 | tf_op jit(solution)/shard_map/sub | solution.py:96
  391.6 3.0 fusion.57
  395.5 18.1 %all_to_all.111 = bf16[8,2,8192]{2,1,0:T(2,128)(2,1)S(1)} all-to-all(bf16[8,2,8192]{2,1,0:T(2,128)(2,1)S(1)} %reshape.309), channel_id=1, replica_groups=mesh['seq'=8,'head'=4] {'seq'}, dimensions={0} | all-to-all | bytes 524288 | tf_op jit(solution)/shard_map/all_to_all | solution.py:172
  414.2 6.9 %all-gather.17.cloned.1.call-done = bf16[2,1024,1024]{2,1,0:T(8,128)(2,1)} async-done(((bf16[2,32,1024]{2,1,0:T(8,128)(2,1)}), bf16[2,1024,1024]{2,1,0:T(8,128)(2,1)}) %all-gather.17.cloned.1.call-update) | async-done | bytes 4194320 | tf_op jit(solution)/shard_map/all_gather | solution.py:133
  421.1 2.1 multiply_reduce_fusion
  423.3 3.8 fusion.32
  427.6 24.1 %all_to_all.112 = bf16[1,128,3,16,64]{1,4,2,0,3:T(8,128)(2,1)S(1)} all-to-all(bf16[1,128,3,16,64]{1,4,2,0,3:T(8,128)(2,1)S(1)} %copy.89), channel_id=1, replica_groups=mesh['seq'=8,'head'=4] {'seq'}, dimensions={3} | all-to-all | bytes 1572864 | tf_op jit(solution)/shard_map/all_to_all | solution.py:170
  452.5 6.0 %convert_reduce_fusion.1 = (f32[2,1024]{1,0:T(2,128)S(1)}, bf16[2,1024,1024]{1,2,0:T(8,128)(2,1)}) fusion(pred[1024,1024]{0,1:T(8,128)(4,1)S(1)} %iota_compare_fusion, bf16[1,1024,3,2,64]{1,4,3,2,0:T(8,128)(2,1)S(1)} %all_to_all.100), kind=kOutput, calls=%fused_computation.28 | convolution fusion | flops 283116544 | bytes 6823936 | tf_op jit(solution)/shard_map/sub | solution.py:96
  458.5 3.0 fusion.59
  462.4 12.3 %all_to_all.113 = bf16[8,2,8192]{2,1,0:T(2,128)(2,1)S(1)} all-to-all(bf16[8,2,8192]{2,1,0:T(2,128)(2,1)S(1)} %reshape.311), channel_id=1, replica_groups=mesh['seq'=8,'head'=4] {'seq'}, dimensions={0} | all-to-all | bytes 524288 | tf_op jit(solution)/shard_map/all_to_all | solution.py:172
  475.4 2.8 fusion.55
  (120 shorter events, 26.9 us)
Async XLA Ops:
  6.5 62.7 %all-gather.9.cloned.1.call-start = ((), (), s32[]{:S(2)}) async-start(), calls=%async_computation.8 | async-start | bytes 2162688 | tf_op jit(solution)/shard_map/all_gather | solution.py:129
  7.3 125.4 %all-gather.7.cloned.1.call-start = ((), (), s32[]{:S(2)}) async-start(), calls=%async_computation.7 | async-start | bytes 2162688 | tf_op jit(solution)/shard_map/all_gather | solution.py:130
  8.0 182.7 %all-gather.11.cloned.1.call-start = ((), (), s32[]{:S(2)}) async-start(), calls=%async_computation.9 | async-start | bytes 2162688 | tf_op jit(solution)/shard_map/all_gather | solution.py:128
  8.7 277.4 %all-gather.13.cloned.1.call-start = ((), (), s32[]{:S(2)}) async-start(), calls=%async_computation.10 | async-start | bytes 2162688 | tf_op jit(solution)/shard_map/all_gather | solution.py:131
  9.3 343.0 %all-gather.15.cloned.1.call-start = ((), (), s32[]{:S(2)}) async-start(), calls=%async_computation.11 | async-start | bytes 12976128 | tf_op jit(solution)/shard_map/all_gather | solution.py:132
  72.4 60.3 %copy-start = (bf16[1,512,1024]{2,1,0:T(8,128)(2,1)S(1)}, bf16[1,512,1024]{2,1,0:T(8,128)(2,1)}, u32[]{:S(2)}) copy-start(bf16[1,512,1024]{2,1,0:T(8,128)(2,1)} %param.16) | copy-start | bytes 3145732
  72.4 60.2 %copy-start.3 = (f32[1024]{0:T(1024)S(1)}, f32[1024]{0:T(1024)}, u32[]{:S(2)}) copy-start(f32[1024]{0:T(1024)} %param.20) | copy-start | bytes 12292
  73.8 121.7 %all-to-all-start.1 = ((bf16[1,512,16,64]{1,3,0,2:T(8,128)(2,1)}), bf16[1,512,16,64]{1,3,0,2:T(8,128)(2,1)S(1)}, u32[]{:S(2)}, u32[]{:S(2)}) async-start(bf16[1,512,16,64]{1,3,0,2:T(8,128)(2,1)} %bitcast.6), calls=%async_computation.1 | async-start | bytes 2097152 | tf_op jit(solution)/shard_map/all_to_all | solution.py:146
  78.1 343.1 %all-gather.17.cloned.1.call-start = ((), (), s32[]{:S(2)}) async-start(), calls=%async_computation.12 | async-start | bytes 4325376 | tf_op jit(solution)/shard_map/all_gather | solution.py:133
  80.8 109.9 %copy-start.4 = (f32[1024]{0:T(1024)S(1)}, f32[1024]{0:T(1024)}, u32[]{:S(2)}) copy-start(f32[1024]{0:T(1024)} %param.19) | copy-start | bytes 12292
  195.5 32.8 %all-to-all-start = ((bf16[1,512,16,64]{1,3,0,2:T(8,128)(2,1)}), bf16[1,512,16,64]{1,3,0,2:T(8,128)(2,1)S(1)}, u32[]{:S(2)}, u32[]{:S(2)}) async-start(bf16[1,512,16,64]{1,3,0,2:T(8,128)(2,1)} %bitcast.2), calls=%async_computation | async-start | bytes 2097152 | tf_op jit(solution)/shard_map/all_to_all | solution.py:147
  219.8 8.5 %copy-start.1 = (bf16[4096,2,64]{0,2,1:T(8,128)(2,1)}, bf16[4096,2,64]{0,2,1:T(8,128)(2,1)S(1)}, u32[]{:S(2)}) copy-start(bf16[4096,2,64]{0,2,1:T(8,128)(2,1)S(1)} %get-tuple-element.490) | copy-start | bytes 3145732
  230.2 46.0 %copy-start.2 = (f32[2,1024]{1,0:T(2,128)S(1)}, f32[2,1024]{1,0:T(2,128)}, u32[]{:S(2)}) copy-start(f32[2,1024]{1,0:T(2,128)} %param.21) | copy-start | bytes 24580
  272.7 12.7 %all-to-all-start.2 = ((bf16[8,2,8192]{2,1,0:T(2,128)(2,1)}), bf16[8,2,8192]{2,1,0:T(2,128)(2,1)S(1)}, u32[]{:S(2)}, u32[]{:S(2)}) async-start(bf16[8,2,8192]{2,1,0:T(2,128)(2,1)} %reshape.307), calls=%async_computation.2 | async-start | bytes 524288 | tf_op jit(solution)/shard_map/all_to_all | solution.py:159
  357.4 27.3 %all-to-all-start.3 = ((bf16[1,128,3,16,64]{1,4,2,0,3:T(8,128)(2,1)}), bf16[1,128,3,16,64]{1,4,2,0,3:T(8,128)(2,1)S(1)}, u32[]{:S(2)}, u32[]{:S(2)}) async-start(bf16[1,128,3,16,64]{1,4,2,0,3:T(8,128)(2,1)} %copy.82), calls=%async_computation.3 | async-start | bytes 1572864 | tf_op jit(solution)/shard_map/all_to_all | solution.py:170
Sparse Core Ops, SparseCore 0:
  10.2 58.9 all-gather.8
  72.0 60.5 all-gather.6
  135.5 55.0 all-gather.10
  193.4 61.0 all-gather.12
  257.3 94.9 all-gather.14
  355.1 66.0 all-gather.16
where the time goes:
time: 486 us; the launch traced here: 485 us
  waiting for transfers between devices  277 us (57%)
  matrix products  84.7 us (17%)
  blocking collectives  54.5 us (11%)
  other arithmetic  20.5 us (4%)
  local copies, waits for them, and re-layouts  17.5 us (4%)
  starting transfers between devices  16.4 us (3%)
  between operations  13.8 us (3%)
    all_gather x1, waiting for transfers between devices, per_device(): lax.all_gather(layer_qkv, ('seq', 'head'), axis=1, tiled=True)  64 us
    all_gather x1, waiting for transfers between devices, per_device(): lax.all_gather(cross_key, ('seq', 'head'), axis=0, tiled=True)  57.8 us
    all_gather x1, waiting for transfers between devices, per_device(): lax.all_gather(cross_value, ('seq', 'head'), axis=0, tiled=True)  51.9 us
    all_gather x1, waiting for transfers between devices, per_device(): lax.all_gather(cross_query, ('seq', 'head'), axis=0, tiled=True)  51.8 us
    all_to_all x2, blocking collectives, per_device(): lax.all_to_all(mixed, 'seq', split_axis=1, concat_axis=2, tiled=True)  30.4 us
    dot_general x16, matrix products, block_scores(): jnp.einsum('oqi,cqi->qoc', query_row_block, key_tile, preferred_element_t...  28.3 us
    dot_general x8, matrix products, project(): jnp.einsum('...k,kn->...n', left, weight, preferred_element_type=jnp.floa...  26.6 us
    all_to_all x1, blocking collectives, per_device(): lax.all_to_all(grouped, 'seq', split_axis=3, concat_axis=1, tiled=True)  24.1 us
  transfers between devices with their start and end apart: 10, of which 8 were waited for; matrix products, arithmetic and copies ran while one was open for 21% of the time, Pallas kernels for 0%

commit v1 on v0

--- a/solution.py
+++ b/solution.py
@@ -129,7 +129,12 @@
         lax.all_gather(cross_key, ("seq", "head"), axis=0, tiled=True),
         lax.all_gather(cross_value, ("seq", "head"), axis=0, tiled=True),
         lax.all_gather(cross_out, ("seq", "head"), axis=0, tiled=True),
-        lax.all_gather(layer_qkv, ("seq", "head"), axis=1, tiled=True),
+        jnp.concatenate(
+            lax.all_to_all(
+                jnp.stack([layer_qkv] * lax.axis_size(("seq", "head"))), ("seq", "head"), 0, 0
+            ),
+            axis=1,
+        ),
         lax.all_gather(layer_out, ("seq", "head"), axis=1, tiled=True),
     )
     normed_latents = rms_norm(latents, query_gain)

time: 486 us -> 724 us (1.49)
  waiting for transfers between devices: 277 us -> 493 us
  local copies, waits for them, and re-layouts: 17.5 us -> 31.7 us
    all_to_all x1, waiting for transfers between devices: 9.13 us -> 164 us  [per_device(): lax.all_to_all(jnp.stack([layer_qkv] * lax.axis_size(('seq', 'head'))), (...]
    all_gather x1, waiting for transfers between devices: 0.02 us -> 137 us  [per_device(): lax.all_gather(cross_out, ('seq', 'head'), axis=0, tiled=True)]
    all_gather x1 -> x0, waiting for transfers between devices: 64 us -> none  [per_device(): lax.all_gather(layer_qkv, ('seq', 'head'), axis=1, tiled=True)]
    all_to_all x0 -> x1, blocking collectives: none -> 12.5 us  [per_device(): lax.all_to_all(jnp.stack(results), 'seq', split_axis=1, concat_axis=2, ti...]
    slice x0 -> x1, local copies, waits for them, and re-layouts: none -> 8.79 us  [per_device(): qkv = project(normed, gathered[4][layer])]
  transfers between devices with their start and end apart: 10 -> 9, of which waited for: 8 -> 7; matrix products, arithmetic and copies ran while one was open for 21% -> 9% of each run, Pallas kernels for 0% -> 0%
where the time goes in v1:
time: 724 us; the launch traced here: 718 us
  waiting for transfers between devices  493 us (68%)
  matrix products  83.1 us (11%)
  blocking collectives  59.1 us (8%)
  local copies, waits for them, and re-layouts  31.7 us (4%)
  other arithmetic  20.5 us (3%)
  starting transfers between devices  16.5 us (2%)
  between operations  13.5 us (2%)
    all_to_all x1, waiting for transfers between devices, per_device(): lax.all_to_all(jnp.stack([layer_qkv] * lax.axis_size(('seq', 'head'))), (...  164 us
    all_gather x1, waiting for transfers between devices, per_device(): lax.all_gather(cross_out, ('seq', 'head'), axis=0, tiled=True)  137 us
    all_gather x1, waiting for transfers between devices, per_device(): lax.all_gather(cross_key, ('seq', 'head'), axis=0, tiled=True)  58.9 us
    all_gather x1, waiting for transfers between devices, per_device(): lax.all_gather(cross_value, ('seq', 'head'), axis=0, tiled=True)  52.4 us
    all_gather x1, waiting for transfers between devices, per_device(): lax.all_gather(cross_query, ('seq', 'head'), axis=0, tiled=True)  51.8 us
    dot_general x16, matrix products, block_scores(): jnp.einsum('oqi,cqi->qoc', query_row_block, key_tile, preferred_element_t...  28.3 us
    dot_general x8, matrix products, project(): jnp.einsum('...k,kn->...n', left, weight, preferred_element_type=jnp.floa...  23.9 us
    all_to_all x2, blocking collectives, per_device(): lax.all_to_all(mixed, 'seq', split_axis=1, concat_axis=2, tiled=True)  23.6 us
  transfers between devices with their start and end apart: 9, of which 7 were waited for; matrix products, arithmetic and copies ran while one was open for 9% of the time, Pallas kernels for 0%

profile of v1, /device:TPU:0, one launch (start us, length us, event | category | flops | bytes accessed | tf_op | source)
XLA Modules:
  0.0 718.0 jit_solution(2045044767840756438)
XLA Ops:
  6.5 0.7 all-gather.8.cloned.1.call-update
  8.7 1.5 fusion.29
  10.3 58.9 %all-gather.8.cloned.1.call-done = bf16[1024,1024]{1,0:T(8,128)(2,1)} async-done(((bf16[32,1024]{1,0:T(8,128)(2,1)}), bf16[1024,1024]{1,0:T(8,128)(2,1)}) %all-gather.8.cloned.1.call-update) | async-done | bytes 2097168 | tf_op jit(solution)/shard_map/all_gather | solution.py:129
  69.2 3.2 convolution_convert_fusion.2
  72.4 1.3 copy.73
  73.8 4.3 all-to-all-start.1
  78.1 2.1 fusion.20
  80.2 52.4 %all-gather.6.cloned.1.call-done = bf16[1024,1024]{1,0:T(8,128)(2,1)} async-done(((bf16[32,1024]{1,0:T(8,128)(2,1)}), bf16[1024,1024]{1,0:T(8,128)(2,1)}) %all-gather.6.cloned.1.call-update) | async-done | bytes 2097168 | tf_op jit(solution)/shard_map/all_gather | solution.py:130
  132.7 3.9 convolution_convert_fusion.3
  136.6 2.3 copy.70
  138.8 51.8 %all-gather.10.cloned.1.call-done = bf16[1024,1024]{1,0:T(8,128)(2,1)} async-done(((bf16[32,1024]{1,0:T(8,128)(2,1)}), bf16[1024,1024]{1,0:T(8,128)(2,1)}) %all-gather.10.cloned.1.call-update) | async-done | bytes 2097168 | tf_op jit(solution)/shard_map/all_gather | solution.py:128
  190.7 4.8 fusion.39
  195.5 4.3 all-to-all-start
  199.8 1.5 copy.75
  201.4 1.6 squeeze.30
  202.9 16.9 %while.30 = (s32[]{:T(128)}, f32[2,1024]{1,0:T(2,128)S(1)}, bf16[4096,2,64]{0,2,1:T(8,128)(2,1)S(1)}, bf16[1024,2,64]{0,2,1:T(8,128)(2,1)S(1)}, s32[]{:T(128)}, ...) while((s32[]{:T(128)}, f32[2,1024]{1,0:T(2,128)S(1)}, bf16[4096,2,64]{0,2,1:T(8,128)(2,1)S(1)}, ...), condition=%wide.region_4.5_spmd.clone, body=%wide.region_2.4_spmd.clone.sunk | while | flops 137891328 | bytes 1487009 | solution.py:47
  204.0 1.0 fusion.102
  206.1 1.0 fusion.102
  208.2 1.0 fusion.102
  210.3 1.0 fusion.102
  212.4 1.0 fusion.102
  214.5 1.0 fusion.102
  216.6 1.0 fusion.102
  218.8 1.0 fusion.102
  219.8 6.2 all-to-all-done
  226.6 1.3 squeeze.14
  227.9 40.5 %while.31 = (s32[]{:T(128)}, f32[1024,2,64]{0,2,1:T(8,128)S(1)}, f32[1024,2]{0,1:T(2,128)S(1)}, bf16[4096,2,64]{0,2,1:T(8,128)(2,1)}, bf16[4096,2,64]{0,2,1:T(8,...) while((s32[]{:T(128)}, f32[1024,2,64]{0,2,1:T(8,128)S(1)}, ...), condition=%wide.region_7.8_spmd.clone, body=%wide.region_5.7_spmd.clone.sunk | while | flops 276565504 | bytes 6869182 | solution.py:80
  228.9 2.5 convert_reduce_fusion.4
  231.5 1.4 fusion.106
  234.0 2.5 convert_reduce_fusion.4
  236.5 1.4 fusion.106
  239.1 2.5 convert_reduce_fusion.4
  241.6 1.4 fusion.106
  244.1 2.5 convert_reduce_fusion.4
  246.6 1.4 fusion.106
  249.2 2.5 convert_reduce_fusion.4
  251.7 1.4 fusion.106
  254.2 2.5 convert_reduce_fusion.4
  256.8 1.4 fusion.106
  259.3 2.5 convert_reduce_fusion.4
  261.8 1.4 fusion.106
  264.4 2.5 convert_reduce_fusion.4
  266.9 1.4 fusion.106
  269.6 12.5 %all_to_all.116 = bf16[8,2,8192]{2,1,0:T(2,128)(2,1)S(1)} all-to-all(bf16[8,2,8192]{2,1,0:T(2,128)(2,1)S(1)} %reshape.318), channel_id=1, replica_groups=mesh['seq'=8,'head'=4] {'seq'}, dimensions={0} | all-to-all | bytes 524288 | tf_op jit(solution)/shard_map/all_to_all | solution.py:164
  282.1 6.1 stack.5
  288.2 3.9 all-to-all-start.3
  294.0 136.6 %all-gather.12.cloned.1.call-done = bf16[1024,1024]{1,0:T(8,128)(2,1)} async-done(((bf16[32,1024]{1,0:T(8,128)(2,1)}), bf16[1024,1024]{1,0:T(8,128)(2,1)}) %all-gather.12.cloned.1.call-update) | async-done | bytes 2097168 | tf_op jit(solution)/shard_map/all_gather | solution.py:131
  430.6 2.1 multiply_reduce_fusion.1
  432.7 164.2 %all-to-all-done.3 = bf16[32,2,32,3072]{3,2,1,0:T(8,128)(2,1)} async-done(((bf16[32,2,32,3072]{3,2,1,0:T(8,128)(2,1)}), bf16[32,2,32,3072]{3,2,1,0:T(8,128)(2,1)}, u32[]{:S(2)}, u32[]{:S(2)}) %all-to-all-start.3) | async-done | bytes 12582944 | tf_op jit(solution)/shard_map/all_to_all | solution.py:133
  596.9 8.8 %fusion.77 = (bf16[1,32,32,3072]{3,2,0,1:T(8,128)(2,1)}, bf16[1,32,32,3072]{3,2,0,1:T(8,128)(2,1)S(1)}) fusion(bf16[2,32,32,3072]{3,2,0,1:T(8,128)(2,1)} %bitcast.20), kind=kLoop, calls=%fused_computation.116 | loop fusion | bytes 25165824 | tf_op jit(solution)/shard_map/slice | solution.py:172
  605.7 1.1 convolution_convert_fusion.1
  607.1 0.9 copy.82
  608.1 3.8 all-to-all-start.4
  612.2 19.5 %all-to-all-done.4 = bf16[1,128,3,16,64]{1,4,2,0,3:T(8,128)(2,1)S(1)} async-done(((bf16[1,128,3,16,64]{1,4,2,0,3:T(8,128)(2,1)}), bf16[1,128,3,16,64]{1,4,2,0,3:T(8,128)(2,1)S(1)}, u32[]{:S(2)}, u32[]{:S(2)}) %all-to-all-start.4) | async-done | bytes 786464 | tf_op jit(solution)/shard_map/all_to_all | solution.py:175
  632.5 6.0 convert_reduce_fusion.2
  638.5 3.0 fusion.53
  642.3 11.7 %all_to_all.117 = bf16[8,2,8192]{2,1,0:T(2,128)(2,1)S(1)} all-to-all(bf16[8,2,8192]{2,1,0:T(2,128)(2,1)S(1)} %reshape.320), channel_id=1, replica_groups=mesh['seq'=8,'head'=4] {'seq'}, dimensions={0} | all-to-all | bytes 524288 | tf_op jit(solution)/shard_map/all_to_all | solution.py:177
  654.8 2.1 multiply_reduce_fusion
  656.9 3.8 convolution_convert_fusion
  661.2 22.9 %all_to_all.118 = bf16[1,128,3,16,64]{1,4,2,0,3:T(8,128)(2,1)S(1)} all-to-all(bf16[1,128,3,16,64]{1,4,2,0,3:T(8,128)(2,1)S(1)} %copy.89), channel_id=1, replica_groups=mesh['seq'=8,'head'=4] {'seq'}, dimensions={3} | all-to-all | bytes 1572864 | tf_op jit(solution)/shard_map/all_to_all | solution.py:175
  685.0 7.3 %convert_reduce_fusion.1 = (f32[2,1024]{1,0:T(2,128)S(1)}, bf16[2,1024,1024]{1,2,0:T(8,128)(2,1)}) fusion(pred[1024,1024]{0,1:T(8,128)(4,1)} %copy-done.2, bf16[1,1024,3,2,64]{1,4,3,2,0:T(8,128)(2,1)S(1)} %all_to_all.104), kind=kOutput, calls=%fused_computation.28 | convolution fusion | flops 283116544 | bytes 6823936 | tf_op jit(solution)/shard_map/sub | solution.py:96
  692.3 3.0 fusion.55
  696.1 11.9 %all_to_all.119 = bf16[8,2,8192]{2,1,0:T(2,128)(2,1)S(1)} all-to-all(bf16[8,2,8192]{2,1,0:T(2,128)(2,1)S(1)} %reshape.322), channel_id=1, replica_groups=mesh['seq'=8,'head'=4] {'seq'}, dimensions={0} | all-to-all | bytes 524288 | tf_op jit(solution)/shard_map/all_to_all | solution.py:177
  708.7 2.8 fusion.51
  (124 shorter events, 27.4 us)
Async XLA Ops:
  6.5 62.7 %all-gather.8.cloned.1.call-start = ((), (), s32[]{:S(2)}) async-start(), calls=%async_computation.9 | async-start | bytes 2162688 | tf_op jit(solution)/shard_map/all_gather | solution.py:129
  7.3 125.4 %all-gather.6.cloned.1.call-start = ((), (), s32[]{:S(2)}) async-start(), calls=%async_computation.8 | async-start | bytes 2162688 | tf_op jit(solution)/shard_map/all_gather | solution.py:130
  8.0 182.7 %all-gather.10.cloned.1.call-start = ((), (), s32[]{:S(2)}) async-start(), calls=%async_computation.10 | async-start | bytes 2162688 | tf_op jit(solution)/shard_map/all_gather | solution.py:128
  72.4 60.2 %copy-start = (bf16[1,512,1024]{2,1,0:T(8,128)(2,1)S(1)}, bf16[1,512,1024]{2,1,0:T(8,128)(2,1)}, u32[]{:S(2)}) copy-start(bf16[1,512,1024]{2,1,0:T(8,128)(2,1)} %param.16) | copy-start | bytes 3145732
  72.4 60.2 %copy-start.5 = (f32[1024]{0:T(1024)S(1)}, f32[1024]{0:T(1024)}, u32[]{:S(2)}) copy-start(f32[1024]{0:T(1024)} %param.20) | copy-start | bytes 12292
  73.8 121.7 %all-to-all-start.1 = ((bf16[1,512,16,64]{1,3,0,2:T(8,128)(2,1)}), bf16[1,512,16,64]{1,3,0,2:T(8,128)(2,1)S(1)}, u32[]{:S(2)}, u32[]{:S(2)}) async-start(bf16[1,512,16,64]{1,3,0,2:T(8,128)(2,1)} %bitcast.6), calls=%async_computation.1 | async-start | bytes 2097152 | tf_op jit(solution)/shard_map/all_to_all | solution.py:151
  80.2 110.4 %copy-start.6 = (f32[1024]{0:T(1024)S(1)}, f32[1024]{0:T(1024)}, u32[]{:S(2)}) copy-start(f32[1024]{0:T(1024)} %param.19) | copy-start | bytes 12292
  195.5 30.5 %all-to-all-start = ((bf16[1,512,16,64]{1,3,0,2:T(8,128)(2,1)}), bf16[1,512,16,64]{1,3,0,2:T(8,128)(2,1)S(1)}, u32[]{:S(2)}, u32[]{:S(2)}) async-start(bf16[1,512,16,64]{1,3,0,2:T(8,128)(2,1)} %bitcast.2), calls=%async_computation | async-start | bytes 2097152 | tf_op jit(solution)/shard_map/all_to_all | solution.py:152
  219.8 6.2 copy-start.1
  268.4 13.8 %copy-start.3 = (bf16[2,32,3072]{2,1,0:T(8,128)(2,1)S(1)}, bf16[2,32,3072]{2,1,0:T(8,128)(2,1)}, u32[]{:S(2)}) copy-start(bf16[2,32,3072]{2,1,0:T(8,128)(2,1)} %param.26) | copy-start | bytes 1179652
  288.2 5.1 copy-start.4
  288.2 308.7 %all-to-all-start.3 = ((bf16[32,2,32,3072]{3,2,1,0:T(8,128)(2,1)}), bf16[32,2,32,3072]{3,2,1,0:T(8,128)(2,1)}, u32[]{:S(2)}, u32[]{:S(2)}) async-start(bf16[32,2,32,3072]{3,2,1,0:T(8,128)(2,1)} %stack.5), calls=%async_computation.3 | async-start | bytes 25165824 | tf_op jit(solution)/shard_map/all_to_all | solution.py:133
  292.1 138.5 %all-gather.12.cloned.1.call-start = ((), (), s32[]{:S(2)}) async-start(), calls=%async_computation.11 | async-start | bytes 2162688 | tf_op jit(solution)/shard_map/all_gather | solution.py:131
  292.7 362.1 %all-gather.14.cloned.1.call-start = ((), (), s32[]{:S(2)}) async-start(), calls=%async_computation.12 | async-start | bytes 4325376 | tf_op jit(solution)/shard_map/all_gather | solution.py:138
  608.1 23.6 %all-to-all-start.4 = ((bf16[1,128,3,16,64]{1,4,2,0,3:T(8,128)(2,1)}), bf16[1,128,3,16,64]{1,4,2,0,3:T(8,128)(2,1)S(1)}, u32[]{:S(2)}, u32[]{:S(2)}) async-start(bf16[1,128,3,16,64]{1,4,2,0,3:T(8,128)(2,1)} %copy.82), calls=%async_computation.4 | async-start | bytes 1572864 | tf_op jit(solution)/shard_map/all_to_all | solution.py:175
  612.1 26.4 %copy-start.2 = (pred[1024,1024]{0,1:T(8,128)(4,1)}, pred[1024,1024]{0,1:T(8,128)(4,1)S(1)}, u32[]{:S(2)}) copy-start(pred[1024,1024]{0,1:T(8,128)(4,1)S(1)} %iota_compare_fusion) | copy-start | bytes 3145732
Sparse Core Ops, SparseCore 0:
  10.2 58.9 all-gather.7
  72.0 60.5 all-gather.5
  135.5 55.0 all-gather.9
  295.5 135.0 all-gather.11
  433.3 112.8 all-gather.13
